TPU v7x, 32 devices: a whole 2x2x4 slice. The times are simulated.
32 devices in a mesh: grp: 4 (over y, x), own: 8 (over z, core).
Axes of the slice: x: 2, y: 2, z: 4, core: 2. Of those that a mesh axis runs over, the one named last changes fastest.
Arguments:
- tile_row: int32 [4, 8, 1536], P('grp', 'own'), may hold values from 0 to 7
- pixel_col: int32 [4, 8, 1536], P('grp', 'own'), may hold values from 0 to 16383
- weight: bfloat16 [4, 8, 1536], P('grp', 'own'), may hold values from 0.25 to 4
- counts: int32 [4, 8, 8], P('grp', 'own'), may hold values from 1 to 192
- kernel: float32 [9, 9], replicated, may hold values from 0.01 to 0.05
Outputs:
- smoothed: float32 [64, 16384], P('own', 'grp')
Inputs may be any that keep to these rules, and one draw needn't show every extreme that they name: `counts`: slots past a block's count hold unused values.
All inputs are finite; a program needn't handle non-finite values.
Results may differ from a plain program's by a relative error of at most 0.0012.
Values may be sent and summed in bfloat16 or wider, within the bound.
A program may use at most 64 MiB of HBM per device.

v0:
```python
import functools
import math

import jax
import jax.numpy as jnp
from jax import lax
from jax.experimental import pallas as pl
from jax.experimental.pallas import tpu as pltpu
from jax.sharding import PartitionSpec as P

W = 16384
STRIP = 8
REACH = 4
TAPS = 9
LANES = 256
CHUNK = 1024
MESH = pl.DeviceIdType.MESH


def heat_kernel(
    n_g, n_o, cap, span, row_hbm, col_hbm, weight_hbm, counts_hbm, kern_hbm, out_ref,
    row_ref, col_ref, weight_ref, counts_ref, kern_ref,
    stage, recv, acc, halo_out, halo_in, own_rows, edge_rows, edge_taps,
    load_sem, send_sem, recv_sem, halo_send_sem, halo_recv_sem,
):
    n = n_g * n_o
    me_g, me_o = lax.axis_index("grp"), lax.axis_index("own")
    quarter = out_ref.shape[1]
    slots = row_ref.shape[2]
    tiles = acc.shape[0] // STRIP

    loads = [
        pltpu.make_async_copy(source, target, load_sem.at[k])
        for k, (source, target) in enumerate(
            [
                (row_hbm, row_ref),
                (col_hbm, col_ref),
                (weight_hbm, weight_ref),
                (counts_hbm, counts_ref),
                (kern_hbm, kern_ref),
            ]
        )
    ]
    for load in loads:
        load.start()

    barrier = pltpu.get_barrier_semaphore()

    def offset_place(mine, step, count):
        if count & (count - 1):
            return lax.rem(mine + step, count)
        place, bit = 0, 1
        while bit < count:
            place = place + bit * lax.rem(lax.div(mine, bit) + lax.div(step, bit), 2)
            bit *= 2
        return place

    def mirrored(step, count):
        return lax.rem(count - step, count) if count & (count - 1) else step

    groups = [offset_place(me_g, jnp.int32(u), n_g) for u in range(n_g)]

    def farthest_first(act):
        def ring(r, carry):
            step = n_o - 1 - r
            owner = offset_place(me_o, step, n_o)
            for u in reversed(range(n_g)):
                act(step, u, owner)
            return carry

        lax.fori_loop(0, n_o - 1, ring, 0)
        for u in range(1, n_g):
            act(0, u, me_o)

    farthest_first(
        lambda step, u, owner: pl.semaphore_signal(
            barrier, inc=1, device_id=(groups[u], owner), device_id_type=MESH
        )
    )

    for load in loads:
        load.wait()

    period = math.lcm(cap, 128)
    per = period // cap

    def prepare(k, carry):
        at = pl.ds(pl.multiple_of(k * period, 128), period)
        lane = lax.broadcasted_iota(jnp.int32, (1, period), 1)
        limit = jnp.full((1, period), counts_ref[0, 0, k * per], jnp.int32)
        for j in range(1, per):
            limit = jnp.where(lane >= j * cap, counts_ref[0, 0, k * per + j] + j * cap, limit)
        index = row_ref[0, :, at] * W + col_ref[0, :, at]
        stage[0:1, at] = index.astype(jnp.float32)
        stage[1:2, at] = jnp.where(lane < limit, weight_ref[0, :, at].astype(jnp.float32), 0.0)
        return carry

    lax.fori_loop(0, slots // period, prepare, 0)
    for k in range(halo_in.shape[0]):
        halo_in_zero = jnp.zeros(halo_in.shape[1:], halo_in.dtype)

        @pl.when(me_o == (0 if k == 0 else n_o - 1))
        def _():
            halo_in[k] = halo_in_zero

    acc[...] = jnp.zeros_like(acc)
    upper = lax.broadcasted_iota(jnp.int32, (STRIP, 128), 0) < REACH
    for a in range(REACH):
        for b in range(TAPS):
            edge_taps[a * TAPS + b] = jnp.where(upper, kern_ref[a, b], kern_ref[a + REACH + 1, b])

    def window(owner):
        return pl.ds(pl.multiple_of(lax.div(owner * cap, 128) * 128, 128), span)

    def copy(step, u, owner):
        there = mirrored(step, n_o) * n_g + mirrored(u, n_g)
        return pltpu.make_async_remote_copy(
            src_ref=stage.at[:, window(owner)],
            dst_ref=recv.at[there],
            send_sem=send_sem.at[step * n_g + u],
            recv_sem=recv_sem.at[there],
            device_id=(groups[u], owner),
            device_id_type=MESH,
        )

    def arrival(k):
        return pltpu.make_async_remote_copy(
            src_ref=recv.at[k],
            dst_ref=recv.at[k],
            send_sem=send_sem.at[k],
            recv_sem=recv_sem.at[k],
            device_id=(me_g, me_o),
            device_id_type=MESH,
        )

    pl.semaphore_wait(barrier, n - 1)

    farthest_first(lambda step, u, owner: copy(step, u, owner).start())
    recv[0] = stage[:, window(me_o)]

    offset = lax.rem(me_o * cap, 128)
    first_col = me_g * quarter - REACH

    def onehots(points):
        index = points[0:1].astype(jnp.int32)
        place = lax.broadcasted_iota(jnp.int32, (1, span), 1) - offset
        reach = (index & (W - 1)) - first_col
        used = (place >= 0) & (place < cap) & (reach >= 0) & (reach < quarter + 2 * REACH)
        mass = jnp.where(used, points[1:2], 0.0)
        cell = (reach // LANES) * STRIP + index // W
        lane = reach & (LANES - 1)
        half = jnp.bfloat16
        cell = jnp.where(used, cell, 0).astype(jnp.float32).astype(half)
        lane = lane.astype(jnp.float32).astype(half)
        cell_iota = lax.broadcasted_iota(jnp.int32, (acc.shape[0], span), 0).astype(jnp.float32).astype(half)
        lane_iota = lax.broadcasted_iota(jnp.int32, (LANES, span), 0).astype(jnp.float32).astype(half)
        cells = jnp.where(cell_iota == cell, half(1), half(0))
        lanes = jnp.where(lane_iota == lane, mass.astype(half), half(0))
        return cells, lanes

    def bin_batch(t, carry):
        cells, lanes = [], []
        for u in range(n_g):
            if u == 0:

                @pl.when(t > 0)
                def _():
                    arrival(t * n_g).wait_recv()
            else:
                arrival(t * n_g + u).wait_recv()
        for u in range(n_g):
            a, b = onehots(recv[t * n_g + u])
            cells.append(a)
            lanes.append(b)
        acc[...] += lax.dot_general(
            jnp.concatenate(cells, axis=1),
            jnp.concatenate(lanes, axis=1),
            (((1,), (1,)), ((), ())),
            preferred_element_type=jnp.float32,
        )
        return carry

    lax.fori_loop(0, n_o, bin_batch, 0)

    for t in range(tiles):
        at = pl.ds(t * LANES, LANES)
        heat = acc[t * STRIP : (t + 1) * STRIP, :]
        halo_out[0, :, at] = heat[STRIP - REACH :].astype(jnp.bfloat16)
        halo_out[1, :, at] = heat[:REACH].astype(jnp.bfloat16)

    def halo_copy(side, owner):
        return pltpu.make_async_remote_copy(
            src_ref=halo_out.at[side],
            dst_ref=halo_in.at[side],
            send_sem=halo_send_sem.at[side],
            recv_sem=halo_recv_sem.at[side],
            device_id=(me_g, owner),
            device_id_type=MESH,
        )

    @pl.when(me_o < n_o - 1)
    def _():
        halo_copy(0, me_o + 1).start()

    @pl.when(me_o > 0)
    def _():
        halo_copy(1, me_o - 1).start()

    def sent(k, carry):
        arrival(k).wait_send()
        return carry

    lax.fori_loop(1, n, sent, 0)

    blank = jnp.zeros((REACH, LANES), jnp.float32)

    def shift_own(t, carry):
        heat = acc[pl.ds(pl.multiple_of(t * STRIP, STRIP), STRIP), :]
        framed = jnp.concatenate([blank, heat, blank], axis=0)
        for a in range(TAPS):
            own_rows[a, :, pl.ds(pl.multiple_of(t * LANES, LANES), LANES)] = framed[a : a + STRIP]
        return carry

    lax.fori_loop(0, tiles, shift_own, 0)

    def smooth(j, carry):
        start = pl.multiple_of(j * CHUNK, 128)
        rows = [own_rows[a, :, pl.ds(start, CHUNK + 128)] for a in range(TAPS)]
        total = None
        for b in range(TAPS):
            part = rows[0] * kern_ref[0, b]
            for a in range(1, TAPS):
                part = part + rows[a] * kern_ref[a, b]
            part = part[:, b : b + CHUNK]
            total = part if total is None else total + part
        out_ref[:, pl.ds(start, CHUNK)] = total
        return carry

    lax.fori_loop(0, quarter // CHUNK, smooth, 0)

    @pl.when(me_o > 0)
    def _():
        halo_copy(0, me_o - 1).wait_recv()

    @pl.when(me_o < n_o - 1)
    def _():
        halo_copy(1, me_o + 1).wait_recv()

    def shift_edge(t, carry):
        at = pl.ds(pl.multiple_of(t * LANES, LANES), LANES)
        above = halo_in[0, :, at].astype(jnp.float32)
        below = halo_in[1, :, at].astype(jnp.float32)
        framed = jnp.concatenate([above, blank[: REACH - 1], below], axis=0)
        for a in range(REACH):
            edge_rows[a, :, at] = framed[a : a + STRIP]
        return carry

    lax.fori_loop(0, tiles, shift_edge, 0)

    def smooth_edge(j, carry):
        start = pl.multiple_of(j * CHUNK, 128)
        rows = [edge_rows[a, :, pl.ds(start, CHUNK + 128)] for a in range(REACH)]
        total = out_ref[:, pl.ds(start, CHUNK)]
        for b in range(TAPS):
            part = None
            for a in range(REACH):
                taps = jnp.concatenate([edge_taps[a * TAPS + b]] * (CHUNK // 128 + 1), axis=1)
                term = rows[a] * taps
                part = term if part is None else part + term
            total = total + part[:, b : b + CHUNK]
        out_ref[:, pl.ds(start, CHUNK)] = total
        return carry

    lax.fori_loop(0, quarter // CHUNK, smooth_edge, 0)

    @pl.when(me_o < n_o - 1)
    def _():
        halo_copy(0, me_o + 1).wait_send()

    @pl.when(me_o > 0)
    def _():
        halo_copy(1, me_o - 1).wait_send()


def per_device(tile_row, pixel_col, weight, counts, kernel):
    n_o = lax.axis_size("own")
    n_g = lax.axis_size("grp")
    n = n_g * n_o
    slots = tile_row.shape[2]
    cap = slots // n_o
    quarter = W // n_g
    span = -(-(max(o * cap % 128 for o in range(n_o)) + cap) // 128) * 128
    tiles = -(-(quarter + 2 * REACH) // LANES)
    width = tiles * LANES
    vmem = pl.BlockSpec(memory_space=pltpu.VMEM)
    hbm = pl.BlockSpec(memory_space=pltpu.HBM)
    return pl.pallas_call(
        functools.partial(heat_kernel, n_g, n_o, cap, span),
        out_shape=pltpu.VMEM((STRIP, quarter), jnp.float32),
        in_specs=[hbm] * 5,
        out_specs=vmem,
        scratch_shapes=[
            pltpu.VMEM(tile_row.shape, jnp.int32),
            pltpu.VMEM(pixel_col.shape, jnp.int32),
            pltpu.VMEM(weight.shape, weight.dtype),
            pltpu.SMEM(counts.shape, jnp.int32),
            pltpu.SMEM(kernel.shape, jnp.float32),
            pltpu.VMEM((2, slots), jnp.float32),
            pltpu.VMEM((n, 2, span), jnp.float32),
            pltpu.VMEM((tiles * STRIP, LANES), jnp.float32),
            pltpu.VMEM((2, REACH, width), jnp.bfloat16),
            pltpu.VMEM((2, REACH, width), jnp.bfloat16),
            pltpu.VMEM((TAPS, STRIP, width), jnp.float32),
            pltpu.VMEM((REACH, STRIP, width), jnp.float32),
            pltpu.VMEM((REACH * TAPS, STRIP, 128), jnp.float32),
            pltpu.SemaphoreType.DMA((5,)),
            pltpu.SemaphoreType.DMA((n,)),
            pltpu.SemaphoreType.DMA((n,)),
            pltpu.SemaphoreType.DMA((2,)),
            pltpu.SemaphoreType.DMA((2,)),
        ],
        compiler_params=pltpu.CompilerParams(collective_id=0, has_side_effects=True),
    )(tile_row, pixel_col, weight, counts, kernel)


def solution(mesh):
    placed = (
        P("grp", "own", None),
        P("grp", "own", None),
        P("grp", "own", None),
        P("grp", "own", None),
        P(),
    )
    return jax.shard_map(
        per_device, mesh=mesh, in_specs=placed, out_specs=P("own", "grp"), check_vma=False
    )
```

profile of v0, /device:TPU:1, one launch (start us, length us, event | category | flops | bytes accessed | tf_op | source)
XLA Modules:
  0.0 16.4 jit_solution(1198471867906945226)
XLA Ops:
  0.0 15.8 %shard_map.55 = f32[8,4096]{1,0:T(8,128)S(1)} custom-call(s32[1,1,1536]{2,1,0:T(1,128)} %row_hbm.1, s32[1,1,1536]{2,1,0:T(1,128)} %col_hbm.1, bf16[1,1,1536]{2,1,0:T(2,128)(2,1)} %weight_hbm.1, s32[1,1,8]{2,1,0:T(1,128)} %counts_hbm.1, f32[9,9]{1,0:T(8,128)} %kern_hbm.1), custom_call_target="tpu_custom_call" | custom-call | tf_op jit(solution)/shard_map/pallas_call | solution.py:297
  15.8 0.7 %copy.7 = f32[8,4096]{1,0:T(8,128)} copy(f32[8,4096]{1,0:T(8,128)S(1)} %shard_map.55) | data formatting | bytes 262144
where the time goes:
time: 16.6 us; the launch traced here: 16.4 us
  Pallas kernels  15.8 us (95%)
  local copies, waits for them, and re-layouts  0.66 us (4%)
    pallas_call x1, Pallas kernels, per_device(): pl.pallas_call(functools.partial(heat_kernel, n_g, n_o, cap, span), out_s...  15.8 us
    unnamed x1, local copies, waits for them, and re-layouts  0.66 us

commit v1 on v0

v1 whole, which is shorter than its diff:
```python
import functools
import math

import jax
import jax.numpy as jnp
from jax import lax
from jax.experimental import pallas as pl
from jax.experimental.pallas import tpu as pltpu
from jax.sharding import PartitionSpec as P

W = 16384
STRIP = 8
REACH = 4
TAPS = 9
LANES = 128
DEEP = 16
BATCHES = (8,)
CHUNK = 1024
MESH = pl.DeviceIdType.MESH


def heat_kernel(
    n_g, n_o, cap, span, row_hbm, col_hbm, weight_hbm, counts_hbm, kern_hbm, out_ref,
    row_ref, col_ref, weight_ref, counts_ref, kern_ref,
    stage, recv, acc, halo_out, halo_in, frame, edge, edge_taps,
    load_sem, send_sem, recv_sem, halo_send_sem, halo_recv_sem,
):
    n = n_g * n_o
    cores = 2 if n_o % 2 == 0 else 1
    me_g, me_o = lax.axis_index("grp"), lax.axis_index("own")
    quarter = out_ref.shape[1]
    slots = row_ref.shape[2]
    tiles = acc.shape[0] // STRIP

    loads = [
        pltpu.make_async_copy(source, target, load_sem.at[k])
        for k, (source, target) in enumerate(
            [
                (counts_hbm, counts_ref),
                (row_hbm, row_ref),
                (col_hbm, col_ref),
                (weight_hbm, weight_ref),
                (kern_hbm, kern_ref),
            ]
        )
    ]
    for load in loads:
        load.start()

    barrier = pltpu.get_barrier_semaphore()

    def offset_place(mine, step, count):
        if count & (count - 1):
            return lax.rem(mine + step, count)
        place, bit = 0, 1
        while bit < count:
            place = place + bit * lax.rem(lax.div(mine, bit) + lax.div(step, bit), 2)
            bit *= 2
        return place

    def mirrored(step, count):
        return lax.rem(count - step, count) if count & (count - 1) else step

    groups = [offset_place(me_g, jnp.int32(u), n_g) for u in range(n_g)]

    def everyone(act):
        def ring(owner, carry):
            for g in range(n_g):

                @pl.when((owner != me_o) | (me_g != g))
                def _():
                    act(g, owner)

            return carry

        lax.fori_loop(0, n_o, ring, 0)

    everyone(
        lambda g, owner: pl.semaphore_signal(
            barrier, inc=1, device_id=(g, owner), device_id_type=MESH
        )
    )

    for load in loads[:4]:
        load.wait()

    period = math.lcm(cap, 128)
    per = period // cap

    def prepare(k, carry):
        at = pl.ds(pl.multiple_of(k * period, 128), period)
        lane = lax.broadcasted_iota(jnp.int32, (1, period), 1)
        limit = jnp.full((1, period), counts_ref[0, 0, k * per], jnp.int32)
        for j in range(1, per):
            limit = jnp.where(lane >= j * cap, counts_ref[0, 0, k * per + j] + j * cap, limit)
        reach = col_ref[0, :, at] + REACH
        index = (reach // LANES * STRIP + row_ref[0, :, at]) * LANES + reach % LANES
        stage[0:1, at] = index.astype(jnp.float32)
        stage[1:2, at] = jnp.where(lane < limit, weight_ref[0, :, at].astype(jnp.float32), 0.0)
        return carry

    lax.fori_loop(0, slots // period, prepare, 0, unroll=slots // period <= 8)

    def window(owner):
        return pl.ds(pl.multiple_of(lax.div(owner * cap, 128) * 128, 128), span)

    def offset_of(mine, place, count):
        if count & (count - 1):
            return lax.rem(place - mine + count, count)
        return offset_place(mine, place, count)

    def send(g, owner):
        step, u = offset_of(me_o, owner, n_o), offset_of(me_g, jnp.int32(g), n_g)
        there = mirrored(step, n_o) * n_g + mirrored(u, n_g)
        pltpu.make_async_remote_copy(
            src_ref=stage.at[:, window(owner)],
            dst_ref=recv.at[there],
            send_sem=send_sem.at[step * n_g + u],
            recv_sem=recv_sem.at[there],
            device_id=(g, owner),
            device_id_type=MESH,
        ).start()

    def arrival(k):
        return pltpu.make_async_remote_copy(
            src_ref=recv.at[k],
            dst_ref=recv.at[k],
            send_sem=send_sem.at[k],
            recv_sem=recv_sem.at[k],
            device_id=(me_g, me_o),
            device_id_type=MESH,
        )

    pl.semaphore_wait(barrier, n - 1)
    everyone(send)
    recv[0] = stage[:, window(me_o)]

    acc[...] = jnp.zeros_like(acc)
    for k in range(halo_in.shape[0]):
        halo_in_zero = jnp.zeros(halo_in.shape[1:], halo_in.dtype)

        @pl.when(me_o == (0 if k == 0 else n_o - 1))
        def _():
            halo_in[k] = halo_in_zero

    loads[4].wait()
    upper = lax.broadcasted_iota(jnp.int32, (STRIP, 128), 0) < REACH
    for a in range(REACH):
        for b in range(TAPS):
            edge_taps[a * TAPS + b] = jnp.where(upper, kern_ref[a, b], kern_ref[a + REACH + 1, b])
    frame[...] = jnp.zeros_like(frame)
    edge[...] = jnp.zeros_like(edge)

    offset = lax.rem(me_o * cap, 128)
    half = jnp.bfloat16
    middle = acc.shape[0] // 2
    origin = me_g * (quarter // LANES * STRIP) + middle
    paired = cap % 128 == 64 and span == cap + 64

    def merged(points):
        lane = lax.broadcasted_iota(jnp.int32, (2, 128), 1)
        width = span - 128
        out, rest = [], []
        for p in points:
            out.append(jnp.where(offset == 0, p[:, :width], p[:, 128:]))
            rest.append(jnp.where(offset == 0, p[:, width:], p[:, :128]))
        for x, y in zip(rest[::2], rest[1::2]):
            out.append(jnp.where((lane < 64) == (offset == 0), x, pltpu.roll(y, 64, 1)))
        return jnp.concatenate(out, axis=1)

    def masked(p):
        place = lax.broadcasted_iota(jnp.int32, (2, span), 1) - offset
        return jnp.where((place >= 0) & (place < cap), p, 0.0)

    def onehots(points):
        count = points.shape[1]
        index = points[0:1].astype(jnp.int32)
        cell = (index // LANES - origin).astype(jnp.float32).astype(half)
        lane = (index % LANES).astype(jnp.float32).astype(half)
        cell_iota = lax.broadcasted_iota(jnp.int32, (acc.shape[0], count), 0) - middle
        cell_iota = cell_iota.astype(jnp.float32).astype(half)
        lane_iota = lax.broadcasted_iota(jnp.int32, (LANES, count), 0).astype(jnp.float32).astype(half)
        cells = jnp.where(cell_iota == cell, half(1), half(0))
        lanes = jnp.where(lane_iota == lane, points[1:2].astype(half), half(0))
        return cells, lanes

    def take(steps):
        places = [step * n_g + u for step in steps for u in range(n_g)]
        for place in places:
            if not (isinstance(place, int) and place == 0):
                arrival(place).wait_recv()
        points = [recv[place] for place in places]
        if paired and len(points) % 2 == 0:
            points = merged(points)
        else:
            points = jnp.concatenate([masked(p) for p in points], axis=1)
        cells, lanes = onehots(points)
        acc[...] += lax.dot_general(
            cells, lanes, (((1,), (1,)), ((), ())), preferred_element_type=jnp.float32
        )

    if n_o <= 8:
        done = 0
        for count in BATCHES:
            steps = range(done, min(done + count, n_o))
            if steps:
                take(steps)
            done += count
        if done < n_o:
            take(range(done, n_o))
    else:
        take([0])

        def one_step(step, carry):
            take([step])
            return carry

        lax.fori_loop(1, n_o, one_step, 0)

    for t in range(tiles):
        heat = acc[t * STRIP : (t + 1) * STRIP, :]
        halo_out[0, t * REACH : (t + 1) * REACH, :] = heat[STRIP - REACH :].astype(half)
        halo_out[1, t * REACH : (t + 1) * REACH, :] = heat[:REACH].astype(half)

    def halo_copy(side, owner):
        return pltpu.make_async_remote_copy(
            src_ref=halo_out.at[side],
            dst_ref=halo_in.at[side],
            send_sem=halo_send_sem.at[side],
            recv_sem=halo_recv_sem.at[side],
            device_id=(me_g, owner),
            device_id_type=MESH,
        )

    @pl.when(me_o < n_o - 1)
    def _():
        halo_copy(0, me_o + 1).start()

    @pl.when(me_o > 0)
    def _():
        halo_copy(1, me_o - 1).start()

    def sent(k, carry):
        arrival(k).wait_send()
        return carry

    for t in range(tiles):
        frame[t * DEEP + REACH : t * DEEP + REACH + STRIP, :] = acc[t * STRIP : (t + 1) * STRIP, :]

    count = CHUNK // LANES

    def smooth(j, carry):
        top = j * count * DEEP
        rows = [
            jnp.concatenate(
                [frame[pl.ds(top + k * DEEP + a, STRIP), :] for k in range(count + 1)], axis=1
            )
            for a in range(TAPS)
        ]
        total = None
        for b in range(TAPS):
            part = rows[0] * kern_ref[0, b]
            for a in range(1, TAPS):
                part = part + rows[a] * kern_ref[a, b]
            part = part[:, b : b + CHUNK]
            total = part if total is None else total + part
        out_ref[:, pl.ds(pl.multiple_of(j * CHUNK, 128), CHUNK)] = total
        return carry

    lax.fori_loop(0, quarter // CHUNK, smooth, 0)
    lax.fori_loop(1, n, sent, 0)

    @pl.when(me_o > 0)
    def _():
        halo_copy(0, me_o - 1).wait_recv()

    @pl.when(me_o < n_o - 1)
    def _():
        halo_copy(1, me_o + 1).wait_recv()

    for t in range(tiles):
        edge[t * DEEP : t * DEEP + REACH, :] = halo_in[0, t * REACH : (t + 1) * REACH, :].astype(jnp.float32)
        edge[t * DEEP + 2 * REACH - 1 : t * DEEP + 3 * REACH - 1, :] = halo_in[
            1, t * REACH : (t + 1) * REACH, :
        ].astype(jnp.float32)

    def smooth_edge(j, carry):
        at = pl.ds(pl.multiple_of(j * CHUNK, 128), CHUNK)
        top = j * count * DEEP
        rows = [
            jnp.concatenate(
                [edge[pl.ds(top + k * DEEP + a, STRIP), :] for k in range(count + 1)], axis=1
            )
            for a in range(REACH)
        ]
        total = out_ref[:, at]
        for b in range(TAPS):
            part = None
            for a in range(REACH):
                taps = jnp.concatenate([edge_taps[a * TAPS + b]] * (count + 1), axis=1)
                term = rows[a] * taps
                part = term if part is None else part + term
            total = total + part[:, b : b + CHUNK]
        out_ref[:, at] = total
        return carry

    lax.fori_loop(0, quarter // CHUNK, smooth_edge, 0)

    @pl.when(me_o < n_o - 1)
    def _():
        halo_copy(0, me_o + 1).wait_send()

    @pl.when(me_o > 0)
    def _():
        halo_copy(1, me_o - 1).wait_send()


def per_device(tile_row, pixel_col, weight, counts, kernel):
    n_o = lax.axis_size("own")
    n_g = lax.axis_size("grp")
    n = n_g * n_o
    slots = tile_row.shape[2]
    cap = slots // n_o
    quarter = W // n_g
    span = -(-(max(o * cap % 128 for o in range(n_o)) + cap) // 128) * 128
    tiles = -(-(quarter + 2 * REACH) // LANES)
    edge_rows = -(-tiles * REACH // 16) * 16
    vmem = pl.BlockSpec(memory_space=pltpu.VMEM)
    hbm = pl.BlockSpec(memory_space=pltpu.HBM)
    return pl.pallas_call(
        functools.partial(heat_kernel, n_g, n_o, cap, span),
        out_shape=pltpu.VMEM((STRIP, quarter), jnp.float32),
        in_specs=[hbm] * 5,
        out_specs=vmem,
        scratch_shapes=[
            pltpu.VMEM(tile_row.shape, jnp.int32),
            pltpu.VMEM(pixel_col.shape, jnp.int32),
            pltpu.VMEM(weight.shape, weight.dtype),
            pltpu.SMEM(counts.shape, jnp.int32),
            pltpu.SMEM(kernel.shape, jnp.float32),
            pltpu.VMEM((2, slots), jnp.float32),
            pltpu.VMEM((n, 2, span), jnp.float32),
            pltpu.VMEM((tiles * STRIP, LANES), jnp.float32),
            pltpu.VMEM((2, edge_rows, LANES), jnp.bfloat16),
            pltpu.VMEM((2, edge_rows, LANES), jnp.bfloat16),
            pltpu.VMEM((tiles * DEEP, LANES), jnp.float32),
            pltpu.VMEM((tiles * DEEP, LANES), jnp.float32),
            pltpu.VMEM((REACH * TAPS, STRIP, 128), jnp.float32),
            pltpu.SemaphoreType.DMA((5,)),
            pltpu.SemaphoreType.DMA((n,)),
            pltpu.SemaphoreType.DMA((n,)),
            pltpu.SemaphoreType.DMA((2,)),
            pltpu.SemaphoreType.DMA((2,)),
        ],
        compiler_params=pltpu.CompilerParams(collective_id=0, has_side_effects=True),
    )(tile_row, pixel_col, weight, counts, kernel)


def solution(mesh):
    placed = (
        P("grp", "own", None),
        P("grp", "own", None),
        P("grp", "own", None),
        P("grp", "own", None),
        P(),
    )
    return jax.shard_map(
        per_device, mesh=mesh, in_specs=placed, out_specs=P("own", "grp"), check_vma=False
    )
```

time: 16.6 us -> 15.1 us (0.910)
  Pallas kernels: 15.8 us -> 14.3 us
    pallas_call x1, Pallas kernels: 15.8 us -> 14.3 us  [per_device(): pl.pallas_call(functools.partial(heat_kernel, n_g, n_o, cap, span), out_s...]
where the time goes in v1:
time: 15.1 us; the launch traced here: 14.9 us
  Pallas kernels  14.3 us (95%)
  local copies, waits for them, and re-layouts  0.66 us (4%)
    pallas_call x1, Pallas kernels, per_device(): pl.pallas_call(functools.partial(heat_kernel, n_g, n_o, cap, span), out_s...  14.3 us
    unnamed x1, local copies, waits for them, and re-layouts  0.66 us

profile of v1, /device:TPU:1, one launch (start us, length us, event | category | flops | bytes accessed | tf_op | source)
XLA Modules:
  0.0 14.9 jit_solution(15769858959167080912)
XLA Ops:
  0.0 14.3 %shard_map.55 = f32[8,4096]{1,0:T(8,128)S(1)} custom-call(s32[1,1,1536]{2,1,0:T(1,128)} %row_hbm.1, s32[1,1,1536]{2,1,0:T(1,128)} %col_hbm.1, bf16[1,1,1536]{2,1,0:T(2,128)(2,1)} %weight_hbm.1, s32[1,1,8]{2,1,0:T(1,128)} %counts_hbm.1, f32[9,9]{1,0:T(8,128)} %kern_hbm.1), custom_call_target="tpu_custom_call" | custom-call | tf_op jit(solution)/shard_map/pallas_call | solution.py:330
  14.3 0.7 %copy.7 = f32[8,4096]{1,0:T(8,128)} copy(f32[8,4096]{1,0:T(8,128)S(1)} %shard_map.55) | data formatting | bytes 262144

commit v2 on v0

v2 whole, which is shorter than its diff:
```python
import functools

import jax
import jax.numpy as jnp
from jax import lax
from jax.experimental import pallas as pl
from jax.experimental.pallas import tpu as pltpu
from jax.sharding import PartitionSpec as P

W = 16384
STRIP = 8
REACH = 4
TAPS = 9
LANES = 128
CHUNK = 1024
MESH = pl.DeviceIdType.MESH


def heat_kernel(
    n_g, n_o, cap, row_hbm, col_hbm, weight_hbm, counts_hbm, kern_hbm, out_ref,
    row_ref, col_ref, weight_ref, counts_ref, kern_ref,
    stage, recv, recv_next, acc, acc_next, halo_out, halo_in, below, band,
    load_sem, send_sem, recv_sem, next_send_sem, next_recv_sem, halo_send_sem, halo_recv_sem,
):
    n = n_g * n_o
    me_g, me_o = lax.axis_index("grp"), lax.axis_index("own")
    quarter = out_ref.shape[1]
    slots = row_ref.shape[2]
    tiles = acc.shape[0] // STRIP
    half = jnp.bfloat16

    loads = [
        pltpu.make_async_copy(source, target, load_sem.at[k])
        for k, (source, target) in enumerate(
            [
                (counts_hbm, counts_ref),
                (row_hbm, row_ref),
                (col_hbm, col_ref),
                (weight_hbm, weight_ref),
                (kern_hbm, kern_ref),
            ]
        )
    ]
    for load in loads:
        load.start()

    barrier = pltpu.get_barrier_semaphore()

    def offset_place(mine, step, count):
        if count & (count - 1):
            return lax.rem(mine + step, count)
        place, bit = 0, 1
        while bit < count:
            place = place + bit * lax.rem(lax.div(mine, bit) + lax.div(step, bit), 2)
            bit *= 2
        return place

    def offset_of(mine, place, count):
        if count & (count - 1):
            return lax.rem(place - mine + count, count)
        return offset_place(mine, place, count)

    def mirrored(step, count):
        return lax.rem(count - step, count) if count & (count - 1) else step

    def everyone(act):
        def ring(owner, carry):
            for g in range(n_g):

                @pl.when((owner != me_o) | (me_g != g))
                def _():
                    act(g, owner)

            return carry

        lax.fori_loop(0, n_o, ring, 0)

    everyone(
        lambda g, owner: pl.semaphore_signal(
            barrier, inc=1, device_id=(g, owner), device_id_type=MESH
        )
    )

    for load in loads[:4]:
        load.wait()

    low = lax.broadcasted_iota(jnp.int32, (1, 128), 1) < 64

    def prepare(k, carry):
        lane = lax.broadcasted_iota(jnp.int32, (1, 128), 1)
        codes, masses = [], []
        for v in range(3):
            at = pl.ds(pl.multiple_of(k * 2 * cap + v * 128, 128), 128)
            reach = col_ref[0, :, at] + REACH
            code = (reach // LANES * STRIP + row_ref[0, :, at]) * LANES + reach % LANES
            codes.append(code.astype(jnp.float32))
            first, second = counts_ref[0, 0, 2 * k], counts_ref[0, 0, 2 * k + 1]
            slot = lane + v * 128
            live = slot < jnp.where(slot < cap, first, second + cap)
            masses.append(jnp.where(live, weight_ref[0, :, at].astype(jnp.float32), 0.0))
        stage[2 * k, :, 0:128] = codes[0]
        stage[2 * k, :, 128:256] = masses[0]
        stage[2 * k, :, 256:384] = jnp.where(low, codes[1], pltpu.roll(masses[1], 64, 1))
        stage[2 * k + 1, :, 0:128] = codes[2]
        stage[2 * k + 1, :, 128:256] = masses[2]
        stage[2 * k + 1, :, 256:384] = jnp.where(low, pltpu.roll(codes[1], 64, 1), masses[1])
        return carry

    lax.fori_loop(0, n_o // 2, prepare, 0, unroll=n_o <= 8)

    def send(source, target, sends, recvs):
        def act(g, owner):
            step, u = offset_of(me_o, owner, n_o), offset_of(me_g, jnp.int32(g), n_g)
            there = mirrored(step, n_o) * n_g + mirrored(u, n_g)
            pltpu.make_async_remote_copy(
                src_ref=stage.at[source(owner)],
                dst_ref=target.at[there],
                send_sem=sends.at[step * n_g + u],
                recv_sem=recvs.at[there],
                device_id=(g, owner),
                device_id_type=MESH,
            ).start()

        return act

    def arrival(k):
        return pltpu.make_async_remote_copy(
            src_ref=recv.at[k],
            dst_ref=recv.at[k],
            send_sem=send_sem.at[k],
            recv_sem=recv_sem.at[k],
            device_id=(me_g, me_o),
            device_id_type=MESH,
        )

    def next_arrival(k):
        return pltpu.make_async_remote_copy(
            src_ref=recv_next.at[k],
            dst_ref=recv_next.at[k],
            send_sem=next_send_sem.at[k],
            recv_sem=next_recv_sem.at[k],
            device_id=(me_g, me_o),
            device_id_type=MESH,
        )

    def reads_next(owner):
        return (lax.rem(owner, 2) == 1) & (owner < n_o - 1)

    pl.semaphore_wait(barrier, n - 1)
    everyone(send(lambda owner: owner, recv, send_sem, recv_sem))
    send_next = send(lambda owner: owner + 1, recv_next, next_send_sem, next_recv_sem)

    def next_ring(k, carry):
        owner = 2 * k + 1
        for g in range(n_g):

            @pl.when((owner != me_o) | (me_g != g))
            def _():
                send_next(g, owner)

        return carry

    lax.fori_loop(0, n_o // 2 - 1, next_ring, 0)
    recv[0] = stage[me_o]

    @pl.when(reads_next(me_o))
    def _():
        recv_next[0] = stage[me_o + 1]

    loads[4].wait()

    spot = lax.broadcasted_iota(jnp.int32, (STRIP, 128), 1)
    line = lax.rem(spot, 2 * STRIP)
    line = jnp.where(line < STRIP, line, jnp.where(line < STRIP + REACH, line - STRIP - REACH, line - REACH))
    tap = line - lax.broadcasted_iota(jnp.int32, (STRIP, 128), 0) + REACH
    for b in range(TAPS):
        taps = jnp.zeros((STRIP, 128), jnp.float32)
        for a in range(TAPS):
            taps = jnp.where(tap == a, kern_ref[a, b], taps)
        coarse = taps.astype(half).astype(jnp.float32)
        band[b * STRIP : (b + 1) * STRIP, :] = jnp.where(spot < 4 * STRIP, coarse, taps - coarse)

    for side, edge in ((0, 0), (1, n_o - 1)):

        @pl.when(me_o == edge)
        def _(side=side):
            halo_in[side] = jnp.zeros(halo_in.shape[1:], half)

    origin = me_g * (quarter // LANES * STRIP)

    def merged(points):
        codes, masses = [], []
        for x, y in zip(points[::2], points[1::2]):
            codes += [x[:, 0:128], y[:, 0:128]]
            masses += [x[:, 128:256], y[:, 128:256]]
            x, y = x[:, 256:384], y[:, 256:384]
            codes.append(jnp.where(low, x, pltpu.roll(y, 64, 1)))
            masses.append(jnp.where(low, pltpu.roll(x, 64, 1), y))
        return jnp.concatenate(codes, axis=1), jnp.concatenate(masses, axis=1)

    def binned(points, rows):
        code, mass = merged(points)
        count = code.shape[1]
        middle = tiles * STRIP // 2
        code = code.astype(jnp.int32)
        cell = (code // LANES - (origin + middle)).astype(jnp.float32).astype(half)
        lane = (code % LANES).astype(jnp.float32).astype(half)
        place = lax.broadcasted_iota(jnp.int32, (tiles * rows, count), 0)
        place = place // rows * STRIP + place % rows - middle
        lane_iota = lax.broadcasted_iota(jnp.int32, (LANES, count), 0).astype(jnp.float32).astype(half)
        cells = jnp.where(place.astype(jnp.float32).astype(half) == cell, half(1), half(0))
        lanes = jnp.where(lane_iota == lane, mass.astype(half), half(0))
        return lax.dot_general(
            cells, lanes, (((1,), (1,)), ((), ())), preferred_element_type=jnp.float32
        )

    def take(source, arrive, target, rows):
        if n_o <= 8:
            for k in range(1, n):
                arrive(k).wait_recv()
            target[...] = binned([source[k] for k in range(n)], rows)
        else:
            target[...] = jnp.zeros_like(target)

            def one_step(step, carry):
                for u in range(n_g):

                    @pl.when(step * n_g + u > 0)
                    def _(u=u):
                        arrive(step * n_g + u).wait_recv()

                target[...] += binned([source[step * n_g + u] for u in range(n_g)], rows)
                return carry

            lax.fori_loop(0, n_o, one_step, 0)

    take(recv, arrival, acc, STRIP)

    for t in range(tiles):
        at = pl.ds(t * LANES, LANES)
        heat = acc[t * STRIP : (t + 1) * STRIP, :]
        halo_out[0, :, at] = heat[STRIP - REACH :].astype(half)
        halo_out[1, :, at] = heat[:REACH].astype(half)

    def halo_copy(side, owner):
        return pltpu.make_async_remote_copy(
            src_ref=halo_out.at[side],
            dst_ref=halo_in.at[side],
            send_sem=halo_send_sem.at[side],
            recv_sem=halo_recv_sem.at[side],
            device_id=(me_g, owner),
            device_id_type=MESH,
        )

    even = lax.rem(me_o, 2) == 0
    sends_down, sends_up = me_o < n_o - 1, lax.rem(me_o, 2) == 1

    @pl.when(sends_down)
    def _():
        halo_copy(0, me_o + 1).start()

    @pl.when(sends_up)
    def _():
        halo_copy(1, me_o - 1).start()

    @pl.when(reads_next(me_o))
    def _():
        take(recv_next, next_arrival, acc_next, REACH)
        for t in range(tiles):
            below[:, t * LANES : (t + 1) * LANES] = acc_next[t * REACH : (t + 1) * REACH, :]

    @pl.when(even)
    def _():
        halo_copy(1, me_o + 1).wait_recv()

    @pl.when(even | (me_o == n_o - 1))
    def _():
        below[...] = halo_in[1].astype(jnp.float32)

    @pl.when(me_o > 0)
    def _():
        halo_copy(0, me_o - 1).wait_recv()

    bands = band[...].astype(half)[:, : 8 * STRIP]
    count = CHUNK // LANES

    for j in range(quarter // CHUNK):
        at = slice(j * CHUNK, (j + 1) * CHUNK + LANES)
        heat = jnp.concatenate(
            [acc[t * STRIP : (t + 1) * STRIP, :] for t in range(j * count, (j + 1) * count + 1)], axis=1
        )
        around = jnp.concatenate([halo_in[0, :, at].astype(jnp.float32), below[:, at]], axis=0)
        field = jnp.concatenate([heat, around], axis=0)
        coarse = field.astype(half)
        fine = (field - coarse.astype(jnp.float32)).astype(half)
        parts = lax.dot_general(
            bands,
            jnp.concatenate([coarse, fine, coarse, fine], axis=0),
            (((1,), (0,)), ((), ())),
            preferred_element_type=jnp.float32,
        )
        total = None
        for b in range(TAPS):
            part = parts[b * STRIP : (b + 1) * STRIP, b : b + CHUNK]
            total = part if total is None else total + part
        out_ref[:, j * CHUNK : (j + 1) * CHUNK] = total

    def sent(k, carry):
        arrival(k).wait_send()
        return carry

    lax.fori_loop(1, n, sent, 0)

    def next_sent(k, carry):
        owner = 2 * k + 1
        for g in range(n_g):

            @pl.when((owner != me_o) | (me_g != g))
            def _():
                step, u = offset_of(me_o, owner, n_o), offset_of(me_g, jnp.int32(g), n_g)
                next_arrival(step * n_g + u).wait_send()

        return carry

    lax.fori_loop(0, n_o // 2 - 1, next_sent, 0)

    @pl.when(sends_down)
    def _():
        halo_copy(0, me_o + 1).wait_send()

    @pl.when(sends_up)
    def _():
        halo_copy(1, me_o - 1).wait_send()


def per_device(tile_row, pixel_col, weight, counts, kernel):
    n_o = lax.axis_size("own")
    n_g = lax.axis_size("grp")
    n = n_g * n_o
    slots = tile_row.shape[2]
    cap = slots // n_o
    quarter = W // n_g
    assert cap == 128 + 64 and n_o % 2 == 0 and n_g % 2 == 0 and quarter % CHUNK == 0
    tiles = -(-(quarter + 2 * REACH) // LANES)
    width = tiles * LANES
    vmem = pl.BlockSpec(memory_space=pltpu.VMEM)
    hbm = pl.BlockSpec(memory_space=pltpu.HBM)
    return pl.pallas_call(
        functools.partial(heat_kernel, n_g, n_o, cap),
        out_shape=pltpu.VMEM((STRIP, quarter), jnp.float32),
        in_specs=[hbm] * 5,
        out_specs=vmem,
        scratch_shapes=[
            pltpu.VMEM(tile_row.shape, jnp.int32),
            pltpu.VMEM(pixel_col.shape, jnp.int32),
            pltpu.VMEM(weight.shape, weight.dtype),
            pltpu.SMEM(counts.shape, jnp.int32),
            pltpu.SMEM(kernel.shape, jnp.float32),
            pltpu.VMEM((n_o, 1, 2 * cap), jnp.float32),
            pltpu.VMEM((n, 1, 2 * cap), jnp.float32),
            pltpu.VMEM((n, 1, 2 * cap), jnp.float32),
            pltpu.VMEM((tiles * STRIP, LANES), jnp.float32),
            pltpu.VMEM((tiles * REACH, LANES), jnp.float32),
            pltpu.VMEM((2, REACH, width), jnp.bfloat16),
            pltpu.VMEM((2, REACH, width), jnp.bfloat16),
            pltpu.VMEM((REACH, width), jnp.float32),
            pltpu.VMEM((TAPS * STRIP, 128), jnp.float32),
            pltpu.SemaphoreType.DMA((5,)),
            pltpu.SemaphoreType.DMA((n,)),
            pltpu.SemaphoreType.DMA((n,)),
            pltpu.SemaphoreType.DMA((n,)),
            pltpu.SemaphoreType.DMA((n,)),
            pltpu.SemaphoreType.DMA((2,)),
            pltpu.SemaphoreType.DMA((2,)),
        ],
        compiler_params=pltpu.CompilerParams(collective_id=0, has_side_effects=True),
    )(tile_row, pixel_col, weight, counts, kernel)


def solution(mesh):
    placed = (
        P("grp", "own", None),
        P("grp", "own", None),
        P("grp", "own", None),
        P("grp", "own", None),
        P(),
    )
    return jax.shard_map(
        per_device, mesh=mesh, in_specs=placed, out_specs=P("own", "grp"), check_vma=False
    )
```

time: 16.6 us -> 14.2 us (0.86)
  the two profiles are of different devices: /device:TPU:1 before, /device:TPU:0 now
where the time goes in v2:
time: 14.2 us; the launch traced here: 14 us
  Pallas kernels  13.3 us (94%)
  local copies, waits for them, and re-layouts  0.66 us (5%)
    pallas_call x1, Pallas kernels, per_device(): pl.pallas_call(functools.partial(heat_kernel, n_g, n_o, cap), out_shape=p...  13.3 us
    unnamed x1, local copies, waits for them, and re-layouts  0.66 us

profile of v2, /device:TPU:0, one launch (start us, length us, event | category | flops | bytes accessed | tf_op | source)
XLA Modules:
  0.0 14.0 jit_solution(18393141743011146870)
XLA Ops:
  0.0 13.3 %shard_map.55 = f32[8,4096]{1,0:T(8,128)S(1)} custom-call(s32[1,1,1536]{2,1,0:T(1,128)} %row_hbm.1, s32[1,1,1536]{2,1,0:T(1,128)} %col_hbm.1, bf16[1,1,1536]{2,1,0:T(2,128)(2,1)} %weight_hbm.1, s32[1,1,8]{2,1,0:T(1,128)} %counts_hbm.1, f32[9,9]{1,0:T(8,128)} %kern_hbm.1), custom_call_target="tpu_custom_call" | custom-call | tf_op jit(solution)/shard_map/pallas_call | solution.py:348
  13.4 0.7 %copy.7 = f32[8,4096]{1,0:T(8,128)} copy(f32[8,4096]{1,0:T(8,128)S(1)} %shard_map.55) | data formatting | bytes 262144

commit v3 on v2

--- a/solution.py
+++ b/solution.py
@@ -115,33 +115,26 @@
             pltpu.make_async_remote_copy(
                 src_ref=stage.at[source(owner)],
                 dst_ref=target.at[there],
-                send_sem=sends.at[step * n_g + u],
-                recv_sem=recvs.at[there],
+                send_sem=sends,
+                recv_sem=recvs,
                 device_id=(g, owner),
                 device_id_type=MESH,
             ).start()
 
         return act
 
-    def arrival(k):
+    def all_of(target, count, sends, recvs):
         return pltpu.make_async_remote_copy(
-            src_ref=recv.at[k],
-            dst_ref=recv.at[k],
-            send_sem=send_sem.at[k],
-            recv_sem=recv_sem.at[k],
+            src_ref=target.at[pl.ds(0, count)],
+            dst_ref=target.at[pl.ds(0, count)],
+            send_sem=sends,
+            recv_sem=recvs,
             device_id=(me_g, me_o),
             device_id_type=MESH,
         )
 
-    def next_arrival(k):
-        return pltpu.make_async_remote_copy(
-            src_ref=recv_next.at[k],
-            dst_ref=recv_next.at[k],
-            send_sem=next_send_sem.at[k],
-            recv_sem=next_recv_sem.at[k],
-            device_id=(me_g, me_o),
-            device_id_type=MESH,
-        )
+    arrivals = all_of(recv, n - 1, send_sem, recv_sem)
+    next_arrivals = all_of(recv_next, n - 1, next_send_sem, next_recv_sem)
 
     def reads_next(owner):
         return (lax.rem(owner, 2) == 1) & (owner < n_o - 1)
@@ -214,27 +207,20 @@
             cells, lanes, (((1,), (1,)), ((), ())), preferred_element_type=jnp.float32
         )
 
-    def take(source, arrive, target, rows):
+    def take(source, target, rows):
         if n_o <= 8:
-            for k in range(1, n):
-                arrive(k).wait_recv()
             target[...] = binned([source[k] for k in range(n)], rows)
         else:
             target[...] = jnp.zeros_like(target)
 
             def one_step(step, carry):
-                for u in range(n_g):
-
-                    @pl.when(step * n_g + u > 0)
-                    def _(u=u):
-                        arrive(step * n_g + u).wait_recv()
-
                 target[...] += binned([source[step * n_g + u] for u in range(n_g)], rows)
                 return carry
 
             lax.fori_loop(0, n_o, one_step, 0)
 
-    take(recv, arrival, acc, STRIP)
+    arrivals.wait_recv()
+    take(recv, acc, STRIP)
 
     for t in range(tiles):
         at = pl.ds(t * LANES, LANES)
@@ -265,7 +251,8 @@
 
     @pl.when(reads_next(me_o))
     def _():
-        take(recv_next, next_arrival, acc_next, REACH)
+        next_arrivals.wait_recv()
+        take(recv_next, acc_next, REACH)
         for t in range(tiles):
             below[:, t * LANES : (t + 1) * LANES] = acc_next[t * REACH : (t + 1) * REACH, :]
 
@@ -305,24 +292,16 @@
             total = part if total is None else total + part
         out_ref[:, j * CHUNK : (j + 1) * CHUNK] = total
 
-    def sent(k, carry):
-        arrival(k).wait_send()
-        return carry
-
-    lax.fori_loop(1, n, sent, 0)
-
-    def next_sent(k, carry):
-        owner = 2 * k + 1
-        for g in range(n_g):
-
-            @pl.when((owner != me_o) | (me_g != g))
-            def _():
-                step, u = offset_of(me_o, owner, n_o), offset_of(me_g, jnp.int32(g), n_g)
-                next_arrival(step * n_g + u).wait_send()
-
-        return carry
-
-    lax.fori_loop(0, n_o // 2 - 1, next_sent, 0)
+    arrivals.wait_send()
+    readers = n_g * (n_o // 2 - 1)
+
+    @pl.when(reads_next(me_o))
+    def _():
+        all_of(recv_next, readers - 1, next_send_sem, next_recv_sem).wait_send()
+
+    @pl.when(jnp.logical_not(reads_next(me_o)))
+    def _():
+        all_of(recv_next, readers, next_send_sem, next_recv_sem).wait_send()
 
     @pl.when(sends_down)
     def _():
@@ -366,10 +345,10 @@
             pltpu.VMEM((REACH, width), jnp.float32),
             pltpu.VMEM((TAPS * STRIP, 128), jnp.float32),
             pltpu.SemaphoreType.DMA((5,)),
-            pltpu.SemaphoreType.DMA((n,)),
-            pltpu.SemaphoreType.DMA((n,)),
-            pltpu.SemaphoreType.DMA((n,)),
-            pltpu.SemaphoreType.DMA((n,)),
+            pltpu.SemaphoreType.DMA,
+            pltpu.SemaphoreType.DMA,
+            pltpu.SemaphoreType.DMA,
+            pltpu.SemaphoreType.DMA,
             pltpu.SemaphoreType.DMA((2,)),
             pltpu.SemaphoreType.DMA((2,)),
         ],

time: 14.2 us -> 12.8 us (0.901)
  Pallas kernels: 13.3 us -> 11.9 us
    pallas_call x1, Pallas kernels: 13.3 us -> 11.9 us  [per_device(): pl.pallas_call(functools.partial(heat_kernel, n_g, n_o, cap), out_shape=p...]
where the time goes in v3:
time: 12.8 us; the launch traced here: 12.6 us
  Pallas kernels  11.9 us (93%)
  local copies, waits for them, and re-layouts  0.66 us (5%)
    pallas_call x1, Pallas kernels, per_device(): pl.pallas_call(functools.partial(heat_kernel, n_g, n_o, cap), out_shape=p...  11.9 us
    unnamed x1, local copies, waits for them, and re-layouts  0.66 us

profile of v3, /device:TPU:0, one launch (start us, length us, event | category | flops | bytes accessed | tf_op | source)
XLA Modules:
  0.0 12.6 jit_solution(14717929605835222794)
XLA Ops:
  0.0 11.9 %shard_map.55 = f32[8,4096]{1,0:T(8,128)S(1)} custom-call(s32[1,1,1536]{2,1,0:T(1,128)} %row_hbm.1, s32[1,1,1536]{2,1,0:T(1,128)} %col_hbm.1, bf16[1,1,1536]{2,1,0:T(2,128)(2,1)} %weight_hbm.1, s32[1,1,8]{2,1,0:T(1,128)} %counts_hbm.1, f32[9,9]{1,0:T(8,128)} %kern_hbm.1), custom_call_target="tpu_custom_call" | custom-call | tf_op jit(solution)/shard_map/pallas_call | solution.py:327
  11.9 0.7 %copy.7 = f32[8,4096]{1,0:T(8,128)} copy(f32[8,4096]{1,0:T(8,128)S(1)} %shard_map.55) | data formatting | bytes 262144

commit v4 on v3

v4 whole, which is shorter than its diff:
```python
import functools

import jax
import jax.numpy as jnp
from jax import lax
from jax.experimental import pallas as pl
from jax.experimental.pallas import tpu as pltpu
from jax.sharding import PartitionSpec as P

W = 16384
STRIP = 8
REACH = 4
TAPS = 9
LANES = 128
CHUNK = 1024
MESH = pl.DeviceIdType.MESH


def hops_of(g, n_g):
    total, bit = 0, 1
    while bit < n_g:
        total, bit = total + g // bit % 2, bit * 2
    return total


def heat_kernel(
    n_g, n_o, cap, late, row_hbm, col_hbm, weight_hbm, counts_hbm, kern_hbm, out_ref,
    row_ref, col_ref, weight_ref, counts_ref, kern_ref,
    stage, recv, recv_late, acc, acc_side, halo_out, halo_in, band,
    ready, load_sem, send_sem, recv_sem, late_sem, halo_send_sem, halo_recv_sem,
):
    n = n_g * n_o
    me_g, me_o = lax.axis_index("grp"), lax.axis_index("own")
    quarter = out_ref.shape[1]
    slots = row_ref.shape[2]
    tiles = acc.shape[0] // STRIP
    half = jnp.bfloat16
    side = lax.rem(me_o, 2)

    loads = [
        pltpu.make_async_copy(source, target, load_sem.at[k])
        for k, (source, target) in enumerate(
            [
                (counts_hbm, counts_ref),
                (row_hbm, row_ref),
                (col_hbm, col_ref),
                (weight_hbm, weight_ref),
                (kern_hbm, kern_ref),
            ]
        )
    ]
    for load in loads:
        load.start()

    barrier = pltpu.get_barrier_semaphore()

    def key(g, owner, hops):
        return (hops + lax.div(owner, 2)) * n + owner * n_g + g

    mine = key(me_g, me_o, hops_of(me_g, n_g))

    def everyone(act):
        def ring(owner, carry):
            for g in range(n_g):
                act(g, owner, key(g, owner, hops_of(g, n_g)))
            return carry

        lax.fori_loop(0, n_o, ring, 0)

    def count_earlier(owner, count):
        for g in range(n_g):
            count = count + jnp.where(key(g, owner, hops_of(g, n_g)) < mine, 1, 0)
        return count

    def tell(semaphore, wanted):
        def act(g, owner, other):
            @pl.when(wanted(other))
            def _():
                pl.semaphore_signal(
                    semaphore, inc=1, device_id=(g, owner), device_id_type=MESH
                )

        return act

    everyone(tell(barrier, lambda other: other > mine))
    earlier = lax.fori_loop(0, n_o, count_earlier, jnp.int32(0))

    @pl.when(earlier > 0)
    def _():
        pl.semaphore_wait(barrier, earlier)

    everyone(tell(ready, lambda other: other < mine))

    for load in loads[:4]:
        load.wait()

    low = lax.broadcasted_iota(jnp.int32, (1, 128), 1) < 64

    def prepare(k, carry):
        lane = lax.broadcasted_iota(jnp.int32, (1, 128), 1)
        codes, masses = [], []
        for v in range(3):
            at = pl.ds(pl.multiple_of(k * 2 * cap + v * 128, 128), 128)
            reach = col_ref[0, :, at] + REACH
            code = (reach // LANES * STRIP + row_ref[0, :, at]) * LANES + reach % LANES
            codes.append(code.astype(jnp.float32))
            first, second = counts_ref[0, 0, 2 * k], counts_ref[0, 0, 2 * k + 1]
            slot = lane + v * 128
            live = slot < jnp.where(slot < cap, first, second + cap)
            masses.append(jnp.where(live, weight_ref[0, :, at].astype(jnp.float32), 0.0))
        stage[2 * k + 1, :, 0:128] = codes[0]
        stage[2 * k + 1, :, 128:256] = masses[0]
        stage[2 * k + 1, :, 256:384] = jnp.where(low, codes[1], pltpu.roll(masses[1], 64, 1))
        stage[2 * k + 2, :, 0:128] = codes[2]
        stage[2 * k + 2, :, 128:256] = masses[2]
        stage[2 * k + 2, :, 256:384] = jnp.where(low, pltpu.roll(codes[1], 64, 1), masses[1])
        return carry

    lax.fori_loop(0, n_o // 2, prepare, 0, unroll=n_o <= 8)

    for k in (0, n_o + 1):
        stage[k] = jnp.zeros(stage.shape[1:], jnp.float32)

    spot = me_o * n_g + me_g
    lately = functools.reduce(jnp.logical_or, [spot == k for k in late], False) if late else None

    def pair_of(owner):
        return pl.ds(owner + lax.rem(owner, 2), 2)

    def trio_of(owner):
        return pl.ds(owner, 3)

    def send(window, target, arrived):
        def act(g, owner):
            pltpu.make_async_remote_copy(
                src_ref=stage.at[window(owner)],
                dst_ref=target.at[spot],
                send_sem=send_sem,
                recv_sem=arrived,
                device_id=(g, owner),
                device_id_type=MESH,
            ).start()

        return act

    def when_late(yes, no):
        if lately is None:
            no()
        else:
            pl.when(lately)(yes)
            pl.when(jnp.logical_not(lately))(no)

    def send_to(wanted):
        def loop(act):
            def one(g, owner, other):
                @pl.when(wanted(other))
                def _():
                    act(g, owner)

            everyone(one)

        when_late(
            lambda: loop(send(trio_of, recv_late, late_sem)),
            lambda: loop(send(pair_of, recv, recv_sem)),
        )

    def all_of(target, count):
        return pltpu.make_async_remote_copy(
            src_ref=target.at[pl.ds(0, count)],
            dst_ref=target.at[pl.ds(0, count)],
            send_sem=send_sem,
            recv_sem=recv_sem if target is recv else late_sem,
            device_id=(me_g, me_o),
            device_id_type=MESH,
        )

    send_to(lambda other: other < mine)

    def keep_late():
        recv_late[spot] = stage[trio_of(me_o)]

    def keep():
        recv[spot] = stage[pair_of(me_o)]

    when_late(keep_late, keep)

    @pl.when(earlier < n - 1)
    def _():
        pl.semaphore_wait(ready, n - 1 - earlier)

    send_to(lambda other: other > mine)

    loads[4].wait()

    column = lax.broadcasted_iota(jnp.int32, (STRIP, 128), 1)
    line = lax.rem(column, 2 * STRIP)
    line = jnp.where(line < STRIP, line, jnp.where(line < STRIP + REACH, line - STRIP - REACH, line - REACH))
    tap = line - lax.broadcasted_iota(jnp.int32, (STRIP, 128), 0) + REACH
    for b in range(TAPS):
        taps = jnp.zeros((STRIP, 128), jnp.float32)
        for a in range(TAPS):
            taps = jnp.where(tap == a, kern_ref[a, b], taps)
        coarse = taps.astype(half).astype(jnp.float32)
        band[b * STRIP : (b + 1) * STRIP, :] = jnp.where(column < 4 * STRIP, coarse, taps - coarse)

    origin = me_g * (quarter // LANES * STRIP)

    def merged(points):
        codes, masses = [], []
        for x, y in zip(points[::2], points[1::2]):
            codes += [x[:, 0:128], y[:, 0:128]]
            masses += [x[:, 128:256], y[:, 128:256]]
            x, y = x[:, 256:384], y[:, 256:384]
            codes.append(jnp.where(low, x, pltpu.roll(y, 64, 1)))
            masses.append(jnp.where(low, pltpu.roll(x, 64, 1), y))
        return jnp.concatenate(codes, axis=1), jnp.concatenate(masses, axis=1)

    def binned(points, rows, base=0):
        code, mass = merged(points)
        count = code.shape[1]
        middle = tiles * STRIP // 2
        code = code.astype(jnp.int32)
        cell = (code // LANES - (origin + middle + base)).astype(jnp.float32).astype(half)
        lane = (code % LANES).astype(jnp.float32).astype(half)
        place = lax.broadcasted_iota(jnp.int32, (tiles * rows, count), 0)
        place = place // rows * STRIP + place % rows - middle
        lane_iota = lax.broadcasted_iota(jnp.int32, (LANES, count), 0).astype(jnp.float32).astype(half)
        cells = jnp.where(place.astype(jnp.float32).astype(half) == cell, half(1), half(0))
        lanes = jnp.where(lane_iota == lane, mass.astype(half), half(0))
        return lax.dot_general(
            cells, lanes, (((1,), (1,)), ((), ())), preferred_element_type=jnp.float32
        )

    early = [k for k in range(n) if k not in late]

    def take(target, rows, which, base):
        if n_o <= 8:
            target[...] = binned([recv[k, which] for k in early], rows, base)
        else:
            target[...] = jnp.zeros_like(target)

            def one_step(step, carry):
                target[...] += binned([recv[step * n_g + g, which] for g in range(n_g)], rows, base)
                return carry

            lax.fori_loop(0, n_o, one_step, 0)

    when_late(
        lambda: all_of(recv, len(early)).wait_recv(), lambda: all_of(recv, len(early) - 1).wait_recv()
    )
    take(acc, STRIP, 1 - side, 0)

    for t in range(tiles):
        heat = acc[t * STRIP : (t + 1) * STRIP, :]
        edge = jnp.where(side == 0, heat[STRIP - REACH :], heat[:REACH])
        halo_out[:, t * LANES : (t + 1) * LANES] = edge.astype(half)
    halo = pltpu.make_async_remote_copy(
        src_ref=halo_out,
        dst_ref=halo_in,
        send_sem=halo_send_sem,
        recv_sem=halo_recv_sem,
        device_id=(me_g, me_o + 1 - 2 * side),
        device_id_type=MESH,
    )
    halo.start()

    outermost = (me_o == 0) | (me_o == n_o - 1)

    @pl.when(outermost)
    def _():
        acc_side[...] = jnp.zeros_like(acc_side)

    @pl.when(jnp.logical_not(outermost))
    def _():
        take(acc_side, REACH, side, REACH * (1 - side))

    if late:
        when_late(
            lambda: all_of(recv_late, len(late) - 1).wait_recv() if len(late) > 1 else None,
            lambda: all_of(recv_late, len(late)).wait_recv(),
        )
        acc[...] += binned([recv_late[k, 1] for k in late], STRIP)
        above = binned([recv_late[k, 0] for k in late], REACH, REACH)
        below = binned([recv_late[k, 2] for k in late], REACH)
    halo.wait_recv()

    bands = band[...].astype(half)[:, : 8 * STRIP]
    count = CHUNK // LANES
    fields = []
    for t in range(tiles):
        at, rows = slice(t * LANES, (t + 1) * LANES), slice(t * REACH, (t + 1) * REACH)
        mate, other = halo_in[:, at].astype(jnp.float32), acc_side[rows, :]
        around = jnp.concatenate(
            [jnp.where(side == 0, other, mate), jnp.where(side == 0, mate, other)], axis=0
        )
        if late:
            around = around + jnp.concatenate([above[rows], below[rows]], axis=0)
        fields.append(jnp.concatenate([acc[t * STRIP : (t + 1) * STRIP, :], around], axis=0))

    for j in range(quarter // CHUNK):
        field = jnp.concatenate(fields[j * count : (j + 1) * count + 1], axis=1)
        coarse = field.astype(half)
        fine = (field - coarse.astype(jnp.float32)).astype(half)
        parts = lax.dot_general(
            bands,
            jnp.concatenate([coarse, fine, coarse, fine], axis=0),
            (((1,), (0,)), ((), ())),
            preferred_element_type=jnp.float32,
        )
        total = None
        for b in range(TAPS):
            part = parts[b * STRIP : (b + 1) * STRIP, b : b + CHUNK]
            total = part if total is None else total + part
        out_ref[:, j * CHUNK : (j + 1) * CHUNK] = total

    when_late(
        lambda: all_of(recv_late, n - 1).wait_send(), lambda: all_of(recv, n - 1).wait_send()
    )
    halo.wait_send()


def per_device(tile_row, pixel_col, weight, counts, kernel):
    n_o = lax.axis_size("own")
    n_g = lax.axis_size("grp")
    n = n_g * n_o
    slots = tile_row.shape[2]
    cap = slots // n_o
    quarter = W // n_g
    assert cap == 128 + 64 and n_o % 2 == 0 and n_g % 2 == 0 and quarter % CHUNK == 0
    tiles = -(-(quarter + 2 * REACH) // LANES)
    width = tiles * LANES
    hops = [hops_of(k % n_g, n_g) + k // n_g // 2 for k in range(n)]
    late = [k for k in range(n) if hops[k] == max(hops)] if n_o <= 8 else []
    vmem = pl.BlockSpec(memory_space=pltpu.VMEM)
    hbm = pl.BlockSpec(memory_space=pltpu.HBM)
    return pl.pallas_call(
        functools.partial(heat_kernel, n_g, n_o, cap, late),
        out_shape=pltpu.VMEM((STRIP, quarter), jnp.float32),
        in_specs=[hbm] * 5,
        out_specs=vmem,
        scratch_shapes=[
            pltpu.VMEM(tile_row.shape, jnp.int32),
            pltpu.VMEM(pixel_col.shape, jnp.int32),
            pltpu.VMEM(weight.shape, weight.dtype),
            pltpu.SMEM(counts.shape, jnp.int32),
            pltpu.SMEM(kernel.shape, jnp.float32),
            pltpu.VMEM((n_o + 2, 1, 2 * cap), jnp.float32),
            pltpu.VMEM((n, 2, 1, 2 * cap), jnp.float32),
            pltpu.VMEM((n if late else 1, 3, 1, 2 * cap), jnp.float32),
            pltpu.VMEM((tiles * STRIP, LANES), jnp.float32),
            pltpu.VMEM((tiles * REACH, LANES), jnp.float32),
            pltpu.VMEM((REACH, width), jnp.bfloat16),
            pltpu.VMEM((REACH, width), jnp.bfloat16),
            pltpu.VMEM((TAPS * STRIP, 128), jnp.float32),
            pltpu.SemaphoreType.REGULAR,
            pltpu.SemaphoreType.DMA((5,)),
            pltpu.SemaphoreType.DMA,
            pltpu.SemaphoreType.DMA,
            pltpu.SemaphoreType.DMA,
            pltpu.SemaphoreType.DMA,
            pltpu.SemaphoreType.DMA,
        ],
        compiler_params=pltpu.CompilerParams(collective_id=0, has_side_effects=True),
    )(tile_row, pixel_col, weight, counts, kernel)


def solution(mesh):
    placed = (
        P("grp", "own", None),
        P("grp", "own", None),
        P("grp", "own", None),
        P("grp", "own", None),
        P(),
    )
    return jax.shard_map(
        per_device, mesh=mesh, in_specs=placed, out_specs=P("own", "grp"), check_vma=False
    )
```

time: 12.8 us -> 14 us (1.094)
  the two profiles are of different devices: /device:TPU:0 before, /device:TPU:25 now
where the time goes in v4:
time: 14 us; the launch traced here: 13.8 us
  Pallas kernels  13.1 us (94%)
  local copies, waits for them, and re-layouts  0.66 us (5%)
    pallas_call x1, Pallas kernels, per_device(): pl.pallas_call(functools.partial(heat_kernel, n_g, n_o, cap, late), out_s...  13.1 us
    unnamed x1, local copies, waits for them, and re-layouts  0.66 us

profile of v4, /device:TPU:25, one launch (start us, length us, event | category | flops | bytes accessed | tf_op | source)
XLA Modules:
  0.0 13.8 jit_solution(1265721838381915184)
XLA Ops:
  0.0 13.1 %shard_map.55 = f32[8,4096]{1,0:T(8,128)S(1)} custom-call(s32[1,1,1536]{2,1,0:T(1,128)} %row_hbm.1, s32[1,1,1536]{2,1,0:T(1,128)} %col_hbm.1, bf16[1,1,1536]{2,1,0:T(2,128)(2,1)} %weight_hbm.1, s32[1,1,8]{2,1,0:T(1,128)} %counts_hbm.1, f32[9,9]{1,0:T(8,128)} %kern_hbm.1), custom_call_target="tpu_custom_call" | custom-call | tf_op jit(solution)/shard_map/pallas_call | solution.py:336
  13.1 0.7 %copy.7 = f32[8,4096]{1,0:T(8,128)} copy(f32[8,4096]{1,0:T(8,128)S(1)} %shard_map.55) | data formatting | bytes 262144

commit v5 on v4

--- a/solution.py
+++ b/solution.py
@@ -14,6 +14,7 @@
 LANES = 128
 CHUNK = 1024
 MESH = pl.DeviceIdType.MESH
+DOWN = False
 
 
 def hops_of(g, n_g):
@@ -26,16 +27,16 @@
 def heat_kernel(
     n_g, n_o, cap, late, row_hbm, col_hbm, weight_hbm, counts_hbm, kern_hbm, out_ref,
     row_ref, col_ref, weight_ref, counts_ref, kern_ref,
-    stage, recv, recv_late, acc, acc_side, halo_out, halo_in, band,
-    ready, load_sem, send_sem, recv_sem, late_sem, halo_send_sem, halo_recv_sem,
+    stage, recv, recv_side, recv_late, acc, acc_side, halo_out, halo_in, band,
+    ready, load_sem, send_sem, recv_sem, side_send_sem, side_recv_sem, late_sem, halo_send_sem, halo_recv_sem,
 ):
     n = n_g * n_o
     me_g, me_o = lax.axis_index("grp"), lax.axis_index("own")
+    side = lax.rem(me_o, 2)
     quarter = out_ref.shape[1]
     slots = row_ref.shape[2]
     tiles = acc.shape[0] // STRIP
     half = jnp.bfloat16
-    side = lax.rem(me_o, 2)
 
     loads = [
         pltpu.make_async_copy(source, target, load_sem.at[k])
@@ -54,42 +55,85 @@
 
     barrier = pltpu.get_barrier_semaphore()
 
-    def key(g, owner, hops):
-        return (hops + lax.div(owner, 2)) * n + owner * n_g + g
-
-    mine = key(me_g, me_o, hops_of(me_g, n_g))
-
-    def everyone(act):
-        def ring(owner, carry):
+    early = [k for k in range(n) if k not in late]
+    spot = me_o * n_g + me_g
+    none = me_o < 0
+    my_chip = lax.div(me_o, 2)
+
+    def bits(g):
+        return [lax.rem(lax.div(g, 1 << b), 2) for b in range(n_g.bit_length() - 1)]
+
+    def covered(g, by):
+        if n_g & (n_g - 1):
+            return g <= by
+        return functools.reduce(jnp.logical_and, [x <= y for x, y in zip(bits(jnp.int32(g)), bits(by))], me_o >= 0)
+
+    inner = [covered(g, me_g) for g in range(n_g)]
+    outer = [covered(me_g, jnp.int32(g)) for g in range(n_g)]
+    same = [me_g == g for g in range(n_g)]
+
+    def precedes(g, owner):
+        chip = lax.div(owner, 2)
+        return inner[g] & ((chip < my_chip) | ((chip == my_chip) & (jnp.logical_not(same[g]) | (owner < me_o))))
+
+    def follows(g, owner):
+        chip = lax.div(owner, 2)
+        return outer[g] & ((chip > my_chip) | ((chip == my_chip) & (jnp.logical_not(same[g]) | (owner > me_o))))
+
+    def the_rest(g, owner):
+        return jnp.logical_not(precedes(g, owner) | (same[g] & (owner == me_o)))
+
+    lately = functools.reduce(jnp.logical_or, [spot == k for k in late], none)
+
+    def when_late(yes, no):
+        if late:
+            pl.when(lately)(yes)
+            pl.when(jnp.logical_not(lately))(no)
+        else:
+            no()
+
+    def visit(act, wanted, low, high, down=False):
+        def chip(i, carry):
+            z = low + high - 1 - i if down else i
             for g in range(n_g):
-                act(g, owner, key(g, owner, hops_of(g, n_g)))
+                for c in range(2):
+                    owner = 2 * z + c
+
+                    @pl.when(wanted(g, owner))
+                    def _(g=g, owner=owner):
+                        act(g, owner)
+
             return carry
 
-        lax.fori_loop(0, n_o, ring, 0)
-
-    def count_earlier(owner, count):
+        lax.fori_loop(low, high, chip, 0)
+
+    def to_earlier(act, also=lambda owner: owner >= 0):
+        visit(act, lambda g, o: precedes(g, o) & also(o), 0, my_chip + 1)
+
+    def to_others(act, also=lambda owner: owner >= 0):
+        visit(act, lambda g, o: the_rest(g, o) & also(o), 0, n_o // 2, DOWN)
+
+    def tell(semaphore):
+        return lambda g, owner: pl.semaphore_signal(
+            semaphore, inc=1, device_id=(g, owner), device_id_type=MESH
+        )
+
+    visit(tell(barrier), follows, my_chip, n_o // 2)
+
+    def count(owner, counts):
+        before, after = counts
         for g in range(n_g):
-            count = count + jnp.where(key(g, owner, hops_of(g, n_g)) < mine, 1, 0)
-        return count
-
-    def tell(semaphore, wanted):
-        def act(g, owner, other):
-            @pl.when(wanted(other))
-            def _():
-                pl.semaphore_signal(
-                    semaphore, inc=1, device_id=(g, owner), device_id_type=MESH
-                )
-
-        return act
-
-    everyone(tell(barrier, lambda other: other > mine))
-    earlier = lax.fori_loop(0, n_o, count_earlier, jnp.int32(0))
+            before = before + jnp.where(precedes(g, owner), 1, 0)
+            after = after + jnp.where(follows(g, owner), 1, 0)
+        return before, after
+
+    earlier, later = lax.fori_loop(0, n_o, count, (jnp.int32(0), jnp.int32(0)), unroll=n_o <= 8)
 
     @pl.when(earlier > 0)
     def _():
         pl.semaphore_wait(barrier, earlier)
 
-    everyone(tell(ready, lambda other: other < mine))
+    to_earlier(tell(ready))
 
     for load in loads[:4]:
         load.wait()
@@ -121,79 +165,66 @@
     for k in (0, n_o + 1):
         stage[k] = jnp.zeros(stage.shape[1:], jnp.float32)
 
-    spot = me_o * n_g + me_g
-    lately = functools.reduce(jnp.logical_or, [spot == k for k in late], False) if late else None
-
-    def pair_of(owner):
-        return pl.ds(owner + lax.rem(owner, 2), 2)
+    def send(source, target, sends, recvs):
+        return lambda g, owner: pltpu.make_async_remote_copy(
+            src_ref=stage.at[source(owner)],
+            dst_ref=target.at[spot],
+            send_sem=sends,
+            recv_sem=recvs,
+            device_id=(g, owner),
+            device_id_type=MESH,
+        ).start()
 
     def trio_of(owner):
         return pl.ds(owner, 3)
 
-    def send(window, target, arrived):
-        def act(g, owner):
-            pltpu.make_async_remote_copy(
-                src_ref=stage.at[window(owner)],
-                dst_ref=target.at[spot],
-                send_sem=send_sem,
-                recv_sem=arrived,
-                device_id=(g, owner),
-                device_id_type=MESH,
-            ).start()
-
-        return act
-
-    def when_late(yes, no):
-        if lately is None:
-            no()
-        else:
-            pl.when(lately)(yes)
-            pl.when(jnp.logical_not(lately))(no)
-
-    def send_to(wanted):
-        def loop(act):
-            def one(g, owner, other):
-                @pl.when(wanted(other))
-                def _():
-                    act(g, owner)
-
-            everyone(one)
-
-        when_late(
-            lambda: loop(send(trio_of, recv_late, late_sem)),
-            lambda: loop(send(pair_of, recv, recv_sem)),
-        )
-
-    def all_of(target, count):
+    def all_of(target, count, sends, recvs):
         return pltpu.make_async_remote_copy(
             src_ref=target.at[pl.ds(0, count)],
             dst_ref=target.at[pl.ds(0, count)],
-            send_sem=send_sem,
-            recv_sem=recv_sem if target is recv else late_sem,
+            send_sem=sends,
+            recv_sem=recvs,
             device_id=(me_g, me_o),
             device_id_type=MESH,
         )
 
-    send_to(lambda other: other < mine)
+    def reads_side(owner):
+        return (owner > 0) & (owner < n_o - 1)
+
+    send_own = send(lambda owner: owner + 1, recv, send_sem, recv_sem)
+    send_side = send(lambda owner: owner + 2 * lax.rem(owner, 2), recv_side, side_send_sem, side_recv_sem)
+    send_trio = send(trio_of, recv_late, send_sem, late_sem)
+
+    when_late(
+        lambda: to_earlier(send_trio),
+        lambda: (to_earlier(send_own), to_earlier(send_side, reads_side))[0],
+    )
 
     def keep_late():
         recv_late[spot] = stage[trio_of(me_o)]
 
-    def keep():
-        recv[spot] = stage[pair_of(me_o)]
-
-    when_late(keep_late, keep)
-
-    @pl.when(earlier < n - 1)
+    def keep_early():
+        recv[spot] = stage[me_o + 1]
+
+        @pl.when(reads_side(me_o))
+        def _():
+            recv_side[spot] = stage[me_o + 2 * side]
+
+    when_late(keep_late, keep_early)
+
+    @pl.when(later > 0)
     def _():
-        pl.semaphore_wait(ready, n - 1 - earlier)
-
-    send_to(lambda other: other > mine)
+        pl.semaphore_wait(ready, later)
+
+    when_late(
+        lambda: to_others(send_trio),
+        lambda: (to_others(send_own), to_others(send_side, reads_side))[0],
+    )
 
     loads[4].wait()
 
-    column = lax.broadcasted_iota(jnp.int32, (STRIP, 128), 1)
-    line = lax.rem(column, 2 * STRIP)
+    spot = lax.broadcasted_iota(jnp.int32, (STRIP, 128), 1)
+    line = lax.rem(spot, 2 * STRIP)
     line = jnp.where(line < STRIP, line, jnp.where(line < STRIP + REACH, line - STRIP - REACH, line - REACH))
     tap = line - lax.broadcasted_iota(jnp.int32, (STRIP, 128), 0) + REACH
     for b in range(TAPS):
@@ -201,7 +232,7 @@
         for a in range(TAPS):
             taps = jnp.where(tap == a, kern_ref[a, b], taps)
         coarse = taps.astype(half).astype(jnp.float32)
-        band[b * STRIP : (b + 1) * STRIP, :] = jnp.where(column < 4 * STRIP, coarse, taps - coarse)
+        band[b * STRIP : (b + 1) * STRIP, :] = jnp.where(spot < 4 * STRIP, coarse, taps - coarse)
 
     origin = me_g * (quarter // LANES * STRIP)
 
@@ -231,24 +262,23 @@
             cells, lanes, (((1,), (1,)), ((), ())), preferred_element_type=jnp.float32
         )
 
-    early = [k for k in range(n) if k not in late]
-
-    def take(target, rows, which, base):
+    def take(source, target, rows, base=0):
         if n_o <= 8:
-            target[...] = binned([recv[k, which] for k in early], rows, base)
+            target[...] = binned([source[k] for k in early], rows, base)
         else:
             target[...] = jnp.zeros_like(target)
 
             def one_step(step, carry):
-                target[...] += binned([recv[step * n_g + g, which] for g in range(n_g)], rows, base)
+                target[...] += binned([source[step * n_g + u] for u in range(n_g)], rows, base)
                 return carry
 
             lax.fori_loop(0, n_o, one_step, 0)
 
     when_late(
-        lambda: all_of(recv, len(early)).wait_recv(), lambda: all_of(recv, len(early) - 1).wait_recv()
-    )
-    take(acc, STRIP, 1 - side, 0)
+        lambda: all_of(recv, len(early), send_sem, recv_sem).wait_recv(),
+        lambda: all_of(recv, len(early) - 1, send_sem, recv_sem).wait_recv(),
+    )
+    take(recv, acc, STRIP)
 
     for t in range(tiles):
         heat = acc[t * STRIP : (t + 1) * STRIP, :]
@@ -264,28 +294,30 @@
     )
     halo.start()
 
-    outermost = (me_o == 0) | (me_o == n_o - 1)
-
-    @pl.when(outermost)
+    @pl.when(reads_side(me_o))
+    def _():
+        when_late(
+            lambda: all_of(recv_side, len(early), side_send_sem, side_recv_sem).wait_recv(),
+            lambda: all_of(recv_side, len(early) - 1, side_send_sem, side_recv_sem).wait_recv(),
+        )
+        take(recv_side, acc_side, REACH, REACH * (1 - side))
+
+    @pl.when(jnp.logical_not(reads_side(me_o)))
     def _():
         acc_side[...] = jnp.zeros_like(acc_side)
 
-    @pl.when(jnp.logical_not(outermost))
-    def _():
-        take(acc_side, REACH, side, REACH * (1 - side))
-
     if late:
-        when_late(
-            lambda: all_of(recv_late, len(late) - 1).wait_recv() if len(late) > 1 else None,
-            lambda: all_of(recv_late, len(late)).wait_recv(),
-        )
+
+        def wait_late():
+            if len(late) > 1:
+                all_of(recv_late, len(late) - 1, send_sem, late_sem).wait_recv()
+
+        when_late(wait_late, lambda: all_of(recv_late, len(late), send_sem, late_sem).wait_recv())
         acc[...] += binned([recv_late[k, 1] for k in late], STRIP)
-        above = binned([recv_late[k, 0] for k in late], REACH, REACH)
-        below = binned([recv_late[k, 2] for k in late], REACH)
+        late_above = binned([recv_late[k, 0] for k in late], REACH, REACH)
+        late_below = binned([recv_late[k, 2] for k in late], REACH)
+
     halo.wait_recv()
-
-    bands = band[...].astype(half)[:, : 8 * STRIP]
-    count = CHUNK // LANES
     fields = []
     for t in range(tiles):
         at, rows = slice(t * LANES, (t + 1) * LANES), slice(t * REACH, (t + 1) * REACH)
@@ -294,8 +326,11 @@
             [jnp.where(side == 0, other, mate), jnp.where(side == 0, mate, other)], axis=0
         )
         if late:
-            around = around + jnp.concatenate([above[rows], below[rows]], axis=0)
+            around = around + jnp.concatenate([late_above[rows], late_below[rows]], axis=0)
         fields.append(jnp.concatenate([acc[t * STRIP : (t + 1) * STRIP, :], around], axis=0))
+
+    bands = band[...].astype(half)[:, : 8 * STRIP]
+    count = CHUNK // LANES
 
     for j in range(quarter // CHUNK):
         field = jnp.concatenate(fields[j * count : (j + 1) * count + 1], axis=1)
@@ -313,9 +348,20 @@
             total = part if total is None else total + part
         out_ref[:, j * CHUNK : (j + 1) * CHUNK] = total
 
-    when_late(
-        lambda: all_of(recv_late, n - 1).wait_send(), lambda: all_of(recv, n - 1).wait_send()
-    )
+    readers = n_g * (n_o - 2)
+
+    def finish_early():
+        all_of(recv, n - 1, send_sem, recv_sem).wait_send()
+
+        @pl.when(reads_side(me_o))
+        def _():
+            all_of(recv_side, readers - 1, side_send_sem, side_recv_sem).wait_send()
+
+        @pl.when(jnp.logical_not(reads_side(me_o)))
+        def _():
+            all_of(recv_side, readers, side_send_sem, side_recv_sem).wait_send()
+
+    when_late(lambda: all_of(recv_late, n - 1, send_sem, late_sem).wait_send(), finish_early)
     halo.wait_send()
 
 
@@ -345,7 +391,8 @@
             pltpu.SMEM(counts.shape, jnp.int32),
             pltpu.SMEM(kernel.shape, jnp.float32),
             pltpu.VMEM((n_o + 2, 1, 2 * cap), jnp.float32),
-            pltpu.VMEM((n, 2, 1, 2 * cap), jnp.float32),
+            pltpu.VMEM((n, 1, 2 * cap), jnp.float32),
+            pltpu.VMEM((n, 1, 2 * cap), jnp.float32),
             pltpu.VMEM((n if late else 1, 3, 1, 2 * cap), jnp.float32),
             pltpu.VMEM((tiles * STRIP, LANES), jnp.float32),
             pltpu.VMEM((tiles * REACH, LANES), jnp.float32),
@@ -359,6 +406,8 @@
             pltpu.SemaphoreType.DMA,
             pltpu.SemaphoreType.DMA,
             pltpu.SemaphoreType.DMA,
+            pltpu.SemaphoreType.DMA,
+            pltpu.SemaphoreType.DMA,
         ],
         compiler_params=pltpu.CompilerParams(collective_id=0, has_side_effects=True),
     )(tile_row, pixel_col, weight, counts, kernel)

time: 14 us -> 12.3 us (0.88)
  the two profiles are of different devices: /device:TPU:25 before, /device:TPU:7 now
where the time goes in v5:
time: 12.3 us; the launch traced here: 12.2 us
  Pallas kernels  11.5 us (93%)
  local copies, waits for them, and re-layouts  0.66 us (5%)
    pallas_call x1, Pallas kernels, per_device(): pl.pallas_call(functools.partial(heat_kernel, n_g, n_o, cap, late), out_s...  11.5 us
    unnamed x1, local copies, waits for them, and re-layouts  0.66 us

profile of v5, /device:TPU:7, one launch (start us, length us, event | category | flops | bytes accessed | tf_op | source)
XLA Modules:
  0.0 12.2 jit_solution(6437138365449604751)
XLA Ops:
  0.0 11.5 %shard_map.55 = f32[8,4096]{1,0:T(8,128)S(1)} custom-call(s32[1,1,1536]{2,1,0:T(1,128)} %row_hbm.1, s32[1,1,1536]{2,1,0:T(1,128)} %col_hbm.1, bf16[1,1,1536]{2,1,0:T(2,128)(2,1)} %weight_hbm.1, s32[1,1,8]{2,1,0:T(1,128)} %counts_hbm.1, f32[9,9]{1,0:T(8,128)} %kern_hbm.1), custom_call_target="tpu_custom_call" | custom-call | tf_op jit(solution)/shard_map/pallas_call | solution.py:382
  11.5 0.7 %copy.7 = f32[8,4096]{1,0:T(8,128)} copy(f32[8,4096]{1,0:T(8,128)S(1)} %shard_map.55) | data formatting | bytes 262144

commit v6 on v5

--- a/solution.py
+++ b/solution.py
@@ -14,7 +14,6 @@
 LANES = 128
 CHUNK = 1024
 MESH = pl.DeviceIdType.MESH
-DOWN = False
 
 
 def hops_of(g, n_g):
@@ -27,7 +26,7 @@
 def heat_kernel(
     n_g, n_o, cap, late, row_hbm, col_hbm, weight_hbm, counts_hbm, kern_hbm, out_ref,
     row_ref, col_ref, weight_ref, counts_ref, kern_ref,
-    stage, recv, recv_side, recv_late, acc, acc_side, halo_out, halo_in, band,
+    stage, recv, recv_side, recv_late, acc, acc_side, acc_mate, halo_out, halo_in, band,
     ready, load_sem, send_sem, recv_sem, side_send_sem, side_recv_sem, late_sem, halo_send_sem, halo_recv_sem,
 ):
     n = n_g * n_o
@@ -72,16 +71,14 @@
     outer = [covered(me_g, jnp.int32(g)) for g in range(n_g)]
     same = [me_g == g for g in range(n_g)]
 
-    def precedes(g, owner):
-        chip = lax.div(owner, 2)
-        return inner[g] & ((chip < my_chip) | ((chip == my_chip) & (jnp.logical_not(same[g]) | (owner < me_o))))
-
-    def follows(g, owner):
-        chip = lax.div(owner, 2)
-        return outer[g] & ((chip > my_chip) | ((chip == my_chip) & (jnp.logical_not(same[g]) | (owner > me_o))))
-
-    def the_rest(g, owner):
-        return jnp.logical_not(precedes(g, owner) | (same[g] & (owner == me_o)))
+    one_if = lambda flag: jnp.where(flag, 1, 0)
+    chips = n_o // 2
+    before = [jnp.where(inner[g], my_chip + 1 - one_if(same[g]), 0) for g in range(n_g)]
+    after = [jnp.where(outer[g], my_chip + one_if(same[g]), chips) for g in range(n_g)]
+    rest = [jnp.where(inner[g], my_chip + 1, 0) for g in range(n_g)]
+    earlier = 2 * sum(before) + side
+    later = 2 * sum(chips - start for start in after) + 1 - side
+    mate = me_o + 1 - 2 * side
 
     lately = functools.reduce(jnp.logical_or, [spot == k for k in late], none)
 
@@ -92,42 +89,35 @@
         else:
             no()
 
-    def visit(act, wanted, low, high, down=False):
-        def chip(i, carry):
-            z = low + high - 1 - i if down else i
+    def visit(act, lows, highs, with_mate):
+        def chip(z, carry):
             for g in range(n_g):
-                for c in range(2):
-                    owner = 2 * z + c
-
-                    @pl.when(wanted(g, owner))
-                    def _(g=g, owner=owner):
-                        act(g, owner)
+
+                @pl.when((z >= lows[g]) & (z < highs[g]))
+                def _(g=g):
+                    for c in range(2):
+                        act(g, 2 * z + c)
 
             return carry
 
-        lax.fori_loop(low, high, chip, 0)
-
-    def to_earlier(act, also=lambda owner: owner >= 0):
-        visit(act, lambda g, o: precedes(g, o) & also(o), 0, my_chip + 1)
-
-    def to_others(act, also=lambda owner: owner >= 0):
-        visit(act, lambda g, o: the_rest(g, o) & also(o), 0, n_o // 2, DOWN)
+        lax.fori_loop(0, chips, chip, 0)
+
+        @pl.when(with_mate)
+        def _():
+            act(me_g, mate)
+
+    def to_earlier(act):
+        visit(act, [0] * n_g, before, side == 1)
+
+    def to_others(act):
+        visit(act, rest, [chips] * n_g, side == 0)
 
     def tell(semaphore):
         return lambda g, owner: pl.semaphore_signal(
             semaphore, inc=1, device_id=(g, owner), device_id_type=MESH
         )
 
-    visit(tell(barrier), follows, my_chip, n_o // 2)
-
-    def count(owner, counts):
-        before, after = counts
-        for g in range(n_g):
-            before = before + jnp.where(precedes(g, owner), 1, 0)
-            after = after + jnp.where(follows(g, owner), 1, 0)
-        return before, after
-
-    earlier, later = lax.fori_loop(0, n_o, count, (jnp.int32(0), jnp.int32(0)), unroll=n_o <= 8)
+    visit(tell(barrier), after, [chips] * n_g, side == 0)
 
     @pl.when(earlier > 0)
     def _():
@@ -193,11 +183,17 @@
 
     send_own = send(lambda owner: owner + 1, recv, send_sem, recv_sem)
     send_side = send(lambda owner: owner + 2 * lax.rem(owner, 2), recv_side, side_send_sem, side_recv_sem)
+
+    def send_beside(g, owner):
+        @pl.when(reads_side(owner))
+        def _():
+            send_side(g, owner)
+
     send_trio = send(trio_of, recv_late, send_sem, late_sem)
 
     when_late(
         lambda: to_earlier(send_trio),
-        lambda: (to_earlier(send_own), to_earlier(send_side, reads_side))[0],
+        lambda: (to_earlier(send_own), to_earlier(send_beside))[0],
     )
 
     def keep_late():
@@ -218,7 +214,7 @@
 
     when_late(
         lambda: to_others(send_trio),
-        lambda: (to_others(send_own), to_others(send_side, reads_side))[0],
+        lambda: (to_others(send_own), to_others(send_beside))[0],
     )
 
     loads[4].wait()
@@ -233,6 +229,12 @@
             taps = jnp.where(tap == a, kern_ref[a, b], taps)
         coarse = taps.astype(half).astype(jnp.float32)
         band[b * STRIP : (b + 1) * STRIP, :] = jnp.where(spot < 4 * STRIP, coarse, taps - coarse)
+
+    acc_mate[...] = jnp.zeros_like(acc_mate)
+
+    @pl.when(jnp.logical_not(reads_side(me_o)))
+    def _():
+        acc_side[...] = jnp.zeros_like(acc_side)
 
     origin = me_g * (quarter // LANES * STRIP)
 
@@ -262,9 +264,9 @@
             cells, lanes, (((1,), (1,)), ((), ())), preferred_element_type=jnp.float32
         )
 
-    def take(source, target, rows, base=0):
+    def take(source, target, rows, base=0, more=()):
         if n_o <= 8:
-            target[...] = binned([source[k] for k in early], rows, base)
+            target[...] = binned([source[k] for k in early] + [recv_late[k, at] for k, at in more], rows, base)
         else:
             target[...] = jnp.zeros_like(target)
 
@@ -274,11 +276,32 @@
 
             lax.fori_loop(0, n_o, one_step, 0)
 
+    first_chip = (me_g == 0) & (me_o < 2)
+
+    def when_first(yes, no):
+        if late:
+            pl.when(first_chip)(yes)
+            pl.when(jnp.logical_not(first_chip))(no)
+        else:
+            no()
+
+    def wait_late():
+        if late:
+            when_late(
+                lambda: all_of(recv_late, len(late) - 1, send_sem, late_sem).wait_recv() if len(late) > 1 else None,
+                lambda: all_of(recv_late, len(late), send_sem, late_sem).wait_recv(),
+            )
+
     when_late(
         lambda: all_of(recv, len(early), send_sem, recv_sem).wait_recv(),
         lambda: all_of(recv, len(early) - 1, send_sem, recv_sem).wait_recv(),
     )
-    take(recv, acc, STRIP)
+
+    def take_all():
+        wait_late()
+        take(recv, acc, STRIP, 0, [(k, 1) for k in late])
+
+    when_first(lambda: take(recv, acc, STRIP), take_all)
 
     for t in range(tiles):
         heat = acc[t * STRIP : (t + 1) * STRIP, :]
@@ -300,33 +323,29 @@
             lambda: all_of(recv_side, len(early), side_send_sem, side_recv_sem).wait_recv(),
             lambda: all_of(recv_side, len(early) - 1, side_send_sem, side_recv_sem).wait_recv(),
         )
-        take(recv_side, acc_side, REACH, REACH * (1 - side))
-
-    @pl.when(jnp.logical_not(reads_side(me_o)))
-    def _():
-        acc_side[...] = jnp.zeros_like(acc_side)
+        base = REACH * (1 - side)
+        when_first(
+            lambda: take(recv_side, acc_side, REACH, base),
+            lambda: take(recv_side, acc_side, REACH, base, [(k, 2 * side) for k in late]),
+        )
 
     if late:
 
-        def wait_late():
-            if len(late) > 1:
-                all_of(recv_late, len(late) - 1, send_sem, late_sem).wait_recv()
-
-        when_late(wait_late, lambda: all_of(recv_late, len(late), send_sem, late_sem).wait_recv())
-        acc[...] += binned([recv_late[k, 1] for k in late], STRIP)
-        late_above = binned([recv_late[k, 0] for k in late], REACH, REACH)
-        late_below = binned([recv_late[k, 2] for k in late], REACH)
+        @pl.when(first_chip)
+        def _():
+            wait_late()
+            acc[...] += binned([recv_late[k, 1] for k in late], STRIP)
+            acc_side[...] += binned([recv_late[k, 2 * side] for k in late], REACH, REACH * (1 - side))
+            acc_mate[...] = binned([recv_late[k, 2 - 2 * side] for k in late], REACH, REACH * side)
 
     halo.wait_recv()
     fields = []
     for t in range(tiles):
         at, rows = slice(t * LANES, (t + 1) * LANES), slice(t * REACH, (t + 1) * REACH)
-        mate, other = halo_in[:, at].astype(jnp.float32), acc_side[rows, :]
+        near, other = halo_in[:, at].astype(jnp.float32) + acc_mate[rows, :], acc_side[rows, :]
         around = jnp.concatenate(
-            [jnp.where(side == 0, other, mate), jnp.where(side == 0, mate, other)], axis=0
-        )
-        if late:
-            around = around + jnp.concatenate([late_above[rows], late_below[rows]], axis=0)
+            [jnp.where(side == 0, other, near), jnp.where(side == 0, near, other)], axis=0
+        )
         fields.append(jnp.concatenate([acc[t * STRIP : (t + 1) * STRIP, :], around], axis=0))
 
     bands = band[...].astype(half)[:, : 8 * STRIP]
@@ -342,11 +361,14 @@
             (((1,), (0,)), ((), ())),
             preferred_element_type=jnp.float32,
         )
-        total = None
-        for b in range(TAPS):
-            part = parts[b * STRIP : (b + 1) * STRIP, b : b + CHUNK]
-            total = part if total is None else total + part
-        out_ref[:, j * CHUNK : (j + 1) * CHUNK] = total
+        for k in range(count):
+            total = parts[:STRIP, k * LANES : (k + 1) * LANES]
+            for b in range(1, TAPS):
+                row = parts[b * STRIP : (b + 1) * STRIP, k * LANES : (k + 2) * LANES]
+                mixed = jnp.where(spot >= b, row[:, :LANES], row[:, LANES:])
+                total = total + pltpu.roll(mixed, LANES - b, 1)
+            at = j * CHUNK + k * LANES
+            out_ref[:, at : at + LANES] = total
 
     readers = n_g * (n_o - 2)
 
@@ -396,6 +418,7 @@
             pltpu.VMEM((n if late else 1, 3, 1, 2 * cap), jnp.float32),
             pltpu.VMEM((tiles * STRIP, LANES), jnp.float32),
             pltpu.VMEM((tiles * REACH, LANES), jnp.float32),
+            pltpu.VMEM((tiles * REACH, LANES), jnp.float32),
             pltpu.VMEM((REACH, width), jnp.bfloat16),
             pltpu.VMEM((REACH, width), jnp.bfloat16),
             pltpu.VMEM((TAPS * STRIP, 128), jnp.float32),

time: 12.3 us -> 12.3 us (level)
  the two profiles are of different devices: /device:TPU:7 before, /device:TPU:5 now
where the time goes in v6:
time: 12.3 us; the launch traced here: 12.2 us
  Pallas kernels  11.5 us (93%)
  local copies, waits for them, and re-layouts  0.66 us (5%)
    pallas_call x1, Pallas kernels, per_device(): pl.pallas_call(functools.partial(heat_kernel, n_g, n_o, cap, late), out_s...  11.5 us
    unnamed x1, local copies, waits for them, and re-layouts  0.66 us

profile of v6, /device:TPU:5, one launch (start us, length us, event | category | flops | bytes accessed | tf_op | source)
XLA Modules:
  0.0 12.2 jit_solution(6253303784631178556)
XLA Ops:
  0.0 11.5 %shard_map.55 = f32[8,4096]{1,0:T(8,128)S(1)} custom-call(s32[1,1,1536]{2,1,0:T(1,128)} %row_hbm.1, s32[1,1,1536]{2,1,0:T(1,128)} %col_hbm.1, bf16[1,1,1536]{2,1,0:T(2,128)(2,1)} %weight_hbm.1, s32[1,1,8]{2,1,0:T(1,128)} %counts_hbm.1, f32[9,9]{1,0:T(8,128)} %kern_hbm.1), custom_call_target="tpu_custom_call" | custom-call | tf_op jit(solution)/shard_map/pallas_call | solution.py:404
  11.5 0.7 %copy.7 = f32[8,4096]{1,0:T(8,128)} copy(f32[8,4096]{1,0:T(8,128)S(1)} %shard_map.55) | data formatting | bytes 262144
